TPU v7x, 256 devices: a whole 4x4x8 slice. The times are simulated.
256 devices in a mesh: row: 16 (over z, core), col: 16 (over y, x).
Axes of the slice: x: 4, y: 4, z: 8, core: 2. Of those that a mesh axis runs over, the one named last changes fastest.
Arguments:
- blocks: bfloat16 [16, 16, 5, 128, 8192], P('row', 'col'), may hold values from -6 to 6
- coords: int32 [16, 16, 5, 3], P('row', 'col'), may hold values from 0 to 15, as said below
- counts: int32 [16, 16], P('row', 'col'), may hold values from 1 to 5, as said below
- doc_factor: bfloat16 [32768, 128], P(('col', 'row')), may hold values from -6 to 6
- ctx_factor: bfloat16 [512, 128], P('col'), may hold values from -0.0625 to 0.0625
Outputs:
- mttkrp: float32 [32768, 128], P(('row', 'col'))
Inputs may be any that keep to these rules, and one draw needn't show every extreme that they name: coords[..., 0] lies in 0 to 15, coords[..., 1] in 0 to 15, coords[..., 2] in 0 to 7; slots at or past the device's count are ignored. `counts`: some device uses all 5 slots.
All inputs are finite; a program needn't handle non-finite values.
Results may differ from a plain program's by a relative error of at most 0.0029.
Values may be sent and summed in bfloat16 or wider, within the bound.
No kernel may reach another device: no remote copies, remote signals or barrier semaphores. Data moves between devices by JAX's collectives and lax.ppermute only.
A program may use at most 64 MiB of HBM per device.

v0:
```python
import jax
import jax.numpy as jnp
from jax import lax
from jax.sharding import PartitionSpec as P

BQ = 128
BD = 128
BK = 64
QBC = 1


def kr_table(brows, crows):
    table = brows[:, None, :].astype(jnp.float32) * crows[None, :, :].astype(jnp.float32)
    return table.reshape(brows.shape[0] * crows.shape[0], brows.shape[1]).astype(jnp.bfloat16)


def body(blocks, coords, counts, doc_factor, ctx_factor):
    doc_slab = lax.all_gather(doc_factor, "row", axis=0, tiled=True)
    ctx_all = lax.all_gather(ctx_factor, "col", axis=0, tiled=True)
    own_blocks = blocks[0, 0]
    own_coords = coords[0, 0]
    used = counts[0, 0]
    rank = doc_slab.shape[1]
    dev_rows = QBC * BQ
    all_rows = dev_rows * lax.axis_size("col")
    start = jnp.int32(0)
    empty = jnp.zeros((all_rows, rank), jnp.float32)

    def step(index, acc):
        place = own_coords[index]
        qstart = place[0] * BQ
        inside = jnp.logical_and(qstart >= start, qstart < start + all_rows)

        def add_term(inner):
            brows = lax.dynamic_slice_in_dim(doc_slab, place[1] * BD, BD, 0)
            crows = lax.dynamic_slice_in_dim(ctx_all, place[2] * BK, BK, 0)
            term = jnp.dot(
                own_blocks[index], kr_table(brows, crows), preferred_element_type=jnp.float32
            )
            local = jnp.clip(qstart, 0, all_rows - BQ)
            current = lax.dynamic_slice_in_dim(inner, local, BQ, 0)
            return lax.dynamic_update_slice_in_dim(inner, current + term, local, 0)

        return lax.cond(inside, add_term, lambda inner: inner, acc)

    partial_value = lax.fori_loop(0, used, step, empty)
    return lax.psum_scatter(partial_value, "col", scatter_dimension=0, tiled=True)


def solution(mesh):
    placed = (
        P("row", "col", None, None, None),
        P("row", "col", None, None),
        P("row", "col"),
        P(("col", "row"), None),
        P("col", None),
    )
    return jax.shard_map(
        body, mesh=mesh, in_specs=placed, out_specs=P(("row", "col"), None), check_vma=False
    )
```

profile of v0, /device:TPU:2, one launch (start us, length us, event | category | flops | bytes accessed | tf_op | source)
XLA Modules:
  0.0 172.4 jit_solution(1418539375337259537)
XLA Ops:
  6.5 23.0 %all_gather.6 = bf16[2048,128]{1,0:T(8,128)(2,1)} all-gather(bf16[128,128]{1,0:T(8,128)(2,1)} %param.12), channel_id=1, replica_groups=mesh['row'=16,'col'=16] {'row'}, dimensions={0}, use_global_device_ids=true | all-gather | bytes 557056 | tf_op jit(solution)/shard_map/all_gather | solution.py:18
  29.6 23.7 %all_gather.7 = bf16[512,128]{1,0:T(8,128)(2,1)S(1)} all-gather(bf16[32,128]{1,0:T(8,128)(2,1)} %param.13), channel_id=1, replica_groups=mesh['row'=16,'col'=16] {'col'}, dimensions={0}, use_global_device_ids=true | all-gather | bytes 139264 | tf_op jit(solution)/shard_map/all_gather | solution.py:19
  53.3 0.8 copy.7
  54.1 35.4 %while.13 = (s32[]{:T(128)}, f32[2048,128]{1,0:T(8,128)S(1)}, s32[]{:T(128)}, s32[5,3]{1,0:T(8,128)S(1)}, bf16[5,128,8192]{2,1,0:T(8,128)(2,1)}, /*index=5*/bf16...) while((s32[]{:T(128)}, f32[2048,128]{1,0:T(8,128)S(1)}, ...), condition=%wide.region_3.4_spmd, body=%wide.region_0.3_spmd.sunk | while | flops 270573568 | bytes 6799827 | solution.py:46
  54.9 6.2 %conditional.2 = (f32[2048,128]{1,0:T(8,128)S(1)}) conditional(s32[]{:T(128)} %convert_element_type.27, f32[2048,128]{1,0:T(8,128)S(1)} %get-tuple-element.150, (s32[]{:T(128)}, f32[2048,128]{1,0:T(8,128)S(1)}, s32[]{:T(128)}, bf16[5,128,8192]{2,1,0:T(8,128)(2,1)}, s32[1,3]{1,0:T(1,128)S(1)}, /*index=5*/bf16[2048,128]{1,0:T(8,128)(2,1)}, ...), branch_computations={%region_1.0_spmd, %region_2.2_spmd} | conditional | flops 270573568 | bytes 6799554 | solution.py:44
  54.9 0.6 fusion.7
  56.1 0.8 dynamic-slice_convert_fusion
  57.6 0.6 multiply_convert_fusion
  58.2 2.3 %fusion.3 = f32[128,128]{1,0:T(8,128)S(1)} fusion(bf16[8192,128]{1,0:T(8,128)(2,1)S(1)} %bitcast.18, bf16[5,128,8192]{2,1,0:T(8,128)(2,1)} %get-tuple-element.54, s32[]{:T(128)S(6)} %select_n.2, f32[2048,128]{1,0:T(8,128)S(1)} %get-tuple-element.52, s32[]{:T(128)S(6)} %min.3), kind=kOutput, calls=%fused_computation.4 | convolution fusion | flops 268451840 | bytes 4325384 | tf_op jit(solution)/shard_map/while/body/cond/branch_1_fun/dot_general | solution.py:37
  60.5 0.6 dynamic_update_slice.2
  61.8 6.2 %conditional.2 = (f32[2048,128]{1,0:T(8,128)S(1)}) conditional(s32[]{:T(128)} %convert_element_type.27, f32[2048,128]{1,0:T(8,128)S(1)} %get-tuple-element.150, (s32[]{:T(128)}, f32[2048,128]{1,0:T(8,128)S(1)}, s32[]{:T(128)}, bf16[5,128,8192]{2,1,0:T(8,128)(2,1)}, s32[1,3]{1,0:T(1,128)S(1)}, /*index=5*/bf16[2048,128]{1,0:T(8,128)(2,1)}, ...), branch_computations={%region_1.0_spmd, %region_2.2_spmd} | conditional | flops 270573568 | bytes 6799554 | solution.py:44
  61.8 0.6 fusion.7
  63.1 0.8 dynamic-slice_convert_fusion
  64.5 0.6 multiply_convert_fusion
  65.2 2.3 %fusion.3 = f32[128,128]{1,0:T(8,128)S(1)} fusion(bf16[8192,128]{1,0:T(8,128)(2,1)S(1)} %bitcast.18, bf16[5,128,8192]{2,1,0:T(8,128)(2,1)} %get-tuple-element.54, s32[]{:T(128)S(6)} %select_n.2, f32[2048,128]{1,0:T(8,128)S(1)} %get-tuple-element.52, s32[]{:T(128)S(6)} %min.3), kind=kOutput, calls=%fused_computation.4 | convolution fusion | flops 268451840 | bytes 4325384 | tf_op jit(solution)/shard_map/while/body/cond/branch_1_fun/dot_general | solution.py:37
  68.8 6.2 %conditional.2 = (f32[2048,128]{1,0:T(8,128)S(1)}) conditional(s32[]{:T(128)} %convert_element_type.27, f32[2048,128]{1,0:T(8,128)S(1)} %get-tuple-element.150, (s32[]{:T(128)}, f32[2048,128]{1,0:T(8,128)S(1)}, s32[]{:T(128)}, bf16[5,128,8192]{2,1,0:T(8,128)(2,1)}, s32[1,3]{1,0:T(1,128)S(1)}, /*index=5*/bf16[2048,128]{1,0:T(8,128)(2,1)}, ...), branch_computations={%region_1.0_spmd, %region_2.2_spmd} | conditional | flops 270573568 | bytes 6799554 | solution.py:44
  68.8 0.6 fusion.7
  70.0 0.8 dynamic-slice_convert_fusion
  71.5 0.6 multiply_convert_fusion
  72.1 2.3 %fusion.3 = f32[128,128]{1,0:T(8,128)S(1)} fusion(bf16[8192,128]{1,0:T(8,128)(2,1)S(1)} %bitcast.18, bf16[5,128,8192]{2,1,0:T(8,128)(2,1)} %get-tuple-element.54, s32[]{:T(128)S(6)} %select_n.2, f32[2048,128]{1,0:T(8,128)S(1)} %get-tuple-element.52, s32[]{:T(128)S(6)} %min.3), kind=kOutput, calls=%fused_computation.4 | convolution fusion | flops 268451840 | bytes 4325384 | tf_op jit(solution)/shard_map/while/body/cond/branch_1_fun/dot_general | solution.py:37
  75.7 6.2 %conditional.2 = (f32[2048,128]{1,0:T(8,128)S(1)}) conditional(s32[]{:T(128)} %convert_element_type.27, f32[2048,128]{1,0:T(8,128)S(1)} %get-tuple-element.150, (s32[]{:T(128)}, f32[2048,128]{1,0:T(8,128)S(1)}, s32[]{:T(128)}, bf16[5,128,8192]{2,1,0:T(8,128)(2,1)}, s32[1,3]{1,0:T(1,128)S(1)}, /*index=5*/bf16[2048,128]{1,0:T(8,128)(2,1)}, ...), branch_computations={%region_1.0_spmd, %region_2.2_spmd} | conditional | flops 270573568 | bytes 6799554 | solution.py:44
  75.7 0.6 fusion.7
  77.0 0.8 dynamic-slice_convert_fusion
  78.4 0.6 multiply_convert_fusion
  79.1 2.3 %fusion.3 = f32[128,128]{1,0:T(8,128)S(1)} fusion(bf16[8192,128]{1,0:T(8,128)(2,1)S(1)} %bitcast.18, bf16[5,128,8192]{2,1,0:T(8,128)(2,1)} %get-tuple-element.54, s32[]{:T(128)S(6)} %select_n.2, f32[2048,128]{1,0:T(8,128)S(1)} %get-tuple-element.52, s32[]{:T(128)S(6)} %min.3), kind=kOutput, calls=%fused_computation.4 | convolution fusion | flops 268451840 | bytes 4325384 | tf_op jit(solution)/shard_map/while/body/cond/branch_1_fun/dot_general | solution.py:37
  82.7 6.2 %conditional.2 = (f32[2048,128]{1,0:T(8,128)S(1)}) conditional(s32[]{:T(128)} %convert_element_type.27, f32[2048,128]{1,0:T(8,128)S(1)} %get-tuple-element.150, (s32[]{:T(128)}, f32[2048,128]{1,0:T(8,128)S(1)}, s32[]{:T(128)}, bf16[5,128,8192]{2,1,0:T(8,128)(2,1)}, s32[1,3]{1,0:T(1,128)S(1)}, /*index=5*/bf16[2048,128]{1,0:T(8,128)(2,1)}, ...), branch_computations={%region_1.0_spmd, %region_2.2_spmd} | conditional | flops 270573568 | bytes 6799554 | solution.py:44
  82.7 0.6 fusion.7
  83.9 0.8 dynamic-slice_convert_fusion
  85.4 0.6 multiply_convert_fusion
  86.0 2.3 %fusion.3 = f32[128,128]{1,0:T(8,128)S(1)} fusion(bf16[8192,128]{1,0:T(8,128)(2,1)S(1)} %bitcast.18, bf16[5,128,8192]{2,1,0:T(8,128)(2,1)} %get-tuple-element.54, s32[]{:T(128)S(6)} %select_n.2, f32[2048,128]{1,0:T(8,128)S(1)} %get-tuple-element.52, s32[]{:T(128)S(6)} %min.3), kind=kOutput, calls=%fused_computation.4 | convolution fusion | flops 268451840 | bytes 4325384 | tf_op jit(solution)/shard_map/while/body/cond/branch_1_fun/dot_general | solution.py:37
  89.6 1.0 copy-done
  90.5 75.0 %reduce-scatter.2.cloned.1.call-done = f32[128,128]{1,0:T(8,128)} async-done(((f32[2048,128]{1,0:T(8,128)}), f32[128,128]{1,0:T(8,128)}) %reduce-scatter.2.cloned.1.call-update) | async-done | bytes 65552 | tf_op jit(solution)/shard_map/reduce_scatter | solution.py:47
  (18 shorter events, 2.5 us)
Async XLA Ops:
  6.5 159.0 %reduce-scatter.2.cloned.1.call-start = ((), (), s32[]{:S(2)}) async-start(), calls=%async_computation.1 | async-start | bytes 1114112 | tf_op jit(solution)/shard_map/reduce_scatter | solution.py:47
  89.5 1.0 copy-start
Sparse Core Ops, SparseCore 0:
  90.7 74.8 reduce-scatter.1
where the time goes:
time: 173 us; the launch traced here: 172 us
  waiting for transfers between devices  75 us (43%)
  blocking collectives  46.8 us (27%)
  between operations  13.4 us (8%)
  matrix products  11.5 us (7%)
  loops' own time  10.9 us (6%)
  local copies, waits for them, and re-layouts  7.87 us (5%)
  other arithmetic  7 us (4%)
    reduce_scatter x1, waiting for transfers between devices, body(): lax.psum_scatter(partial_value, 'col', scatter_dimension=0, tiled=True)  75 us
    all_gather x1, blocking collectives, body(): ctx_all = lax.all_gather(ctx_factor, 'col', axis=0, tiled=True)  23.7 us
    all_gather x1, blocking collectives, body(): doc_slab = lax.all_gather(doc_factor, 'row', axis=0, tiled=True)  23 us
    dot_general x5, matrix products, add_term(): jnp.dot(own_blocks[index], kr_table(brows, crows), preferred_element_type...  11.5 us
    another operation x5, loops' own time, step(): return lax.cond(inside, add_term, lambda inner: inner, acc)  6.59 us
    another operation x1, loops' own time, body(): partial_value = lax.fori_loop(0, used, step, empty)  4.29 us
    convert_element_type x5, other arithmetic, kr_table(): brows[:, None, :].astype(jnp.float32)  3.84 us
  transfers between devices with their start and end apart: 1, of which 1 were waited for; matrix products, arithmetic and copies ran while one was open for 0% of the time, Pallas kernels for 0%

commit v1 on v0

--- a/solution.py
+++ b/solution.py
@@ -16,7 +16,25 @@
 
 def body(blocks, coords, counts, doc_factor, ctx_factor):
     doc_slab = lax.all_gather(doc_factor, "row", axis=0, tiled=True)
-    ctx_all = lax.all_gather(ctx_factor, "col", axis=0, tiled=True)
+    size, here, span = (lax.axis_size("col"), lax.axis_index("col"), ctx_factor.shape[0])
+    right = [(i, (i + 1) % size) for i in range(size)]
+    behind = [(i, (i - 1) % size) for i in range(size)]
+    ctx_all = jnp.zeros(
+        (*ctx_factor.shape[:0], size * span, *ctx_factor.shape[0 + 1 :]), ctx_factor.dtype
+    )
+    ctx_all = lax.dynamic_update_slice_in_dim(ctx_all, ctx_factor, here * span, axis=0)
+    from_left = from_right = ctx_factor
+    half = size // 2
+    for k in range(1, half + 1):
+        from_left = lax.ppermute(from_left, "col", right)
+        ctx_all = lax.dynamic_update_slice_in_dim(
+            ctx_all, from_left, (here - k) % size * span, axis=0
+        )
+        if k < size - half:
+            from_right = lax.ppermute(from_right, "col", behind)
+            ctx_all = lax.dynamic_update_slice_in_dim(
+                ctx_all, from_right, (here + k) % size * span, axis=0
+            )
     own_blocks = blocks[0, 0]
     own_coords = coords[0, 0]
     used = counts[0, 0]

time: 173 us -> 200 us (1.16)
  starting transfers between devices: 0.01 us -> 32.9 us
  blocking collectives: 46.8 us -> 22.8 us
  waiting for transfers between devices: 75 us -> 92.2 us
    ppermute x0 -> x15, starting transfers between devices: none -> 32.9 us  [the longest x7 29.9 us: body(): from_right = lax.ppermute(from_right, 'col', behind)]
    all_gather x1 -> x0, blocking collectives: 23.7 us -> none  [body(): ctx_all = lax.all_gather(ctx_factor, 'col', axis=0, tiled=True)]
    ppermute x0 -> x15, waiting for transfers between devices: none -> 16.5 us  [the longest x8 16.5 us: body(): from_left = lax.ppermute(from_left, 'col', right)]
  transfers between devices with their start and end apart: 1 -> 16, of which waited for: 1 -> 8; matrix products, arithmetic and copies ran while one was open for 0% -> 1% of each run, Pallas kernels for 0% -> 0%
where the time goes in v1:
time: 200 us
  waiting for transfers between devices  92.2 us (46%)
  starting transfers between devices  32.9 us (16%)
  blocking collectives  22.8 us (11%)
  between operations  13.4 us (7%)
  matrix products  11.5 us (6%)
  loops' own time  11.1 us (6%)
  local copies, waits for them, and re-layouts  8.79 us (4%)
  other arithmetic  7 us (4%)
    reduce_scatter x1, waiting for transfers between devices, body(): lax.psum_scatter(partial_value, 'col', scatter_dimension=0, tiled=True)  75.7 us
    ppermute x7, starting transfers between devices, body(): from_right = lax.ppermute(from_right, 'col', behind)  29.9 us
    all_gather x1, blocking collectives, body(): doc_slab = lax.all_gather(doc_factor, 'row', axis=0, tiled=True)  22.8 us
    ppermute x8, waiting for transfers between devices, body(): from_left = lax.ppermute(from_left, 'col', right)  16.5 us
    dot_general x5, matrix products, add_term(): jnp.dot(own_blocks[index], kr_table(brows, crows), preferred_element_type...  11.5 us
    another operation x5, loops' own time, step(): return lax.cond(inside, add_term, lambda inner: inner, acc)  6.76 us
    another operation x1, loops' own time, body(): partial_value = lax.fori_loop(0, used, step, empty)  4.29 us
  transfers between devices with their start and end apart: 16, of which 8 were waited for; matrix products, arithmetic and copies ran while one was open for 1% of the time, Pallas kernels for 0%

profile of v1, /device:TPU:2, one launch (start us, length us, event | category | flops | bytes accessed | tf_op | source)
XLA Modules:
  0.0 199.7 jit_solution(2360566166202746300)
XLA Ops:
  6.5 1.5 collective-permute-start
  8.8 22.8 %all_gather.3 = bf16[2048,128]{1,0:T(8,128)(2,1)} all-gather(bf16[128,128]{1,0:T(8,128)(2,1)} %param.12), channel_id=1, replica_groups=mesh['row'=16,'col'=16] {'row'}, dimensions={0}, use_global_device_ids=true | all-gather | bytes 557056 | tf_op jit(solution)/shard_map/all_gather | solution.py:18
  33.1 1.5 collective-permute-start.2
  34.6 2.5 %collective-permute-start.3 = (bf16[32,128]{1,0:T(8,128)(2,1)S(1)}, bf16[32,128]{1,0:T(8,128)(2,1)S(1)}, u32[]{:S(2)}, u32[]{:S(2)}) collective-permute-start(bf16[32,128]{1,0:T(8,128)(2,1)S(1)} %collective-permute-done.1), channel_id=1, source_target_pairs={{0,15},{1,0},{2,1},{3,2},{4,3},{5,4},{6,5},{7,6},{8,7},{9,8},{10,9... | collective-permute-start | bytes 24584 | tf_op jit(solution)/shard_map/ppermute | solution.py:34
  37.1 1.5 collective-permute-done.2
  38.6 5.3 %collective-permute-start.5 = (bf16[32,128]{1,0:T(8,128)(2,1)S(1)}, bf16[32,128]{1,0:T(8,128)(2,1)S(1)}, u32[]{:S(2)}, u32[]{:S(2)}) collective-permute-start(bf16[32,128]{1,0:T(8,128)(2,1)S(1)} %collective-permute-done.3), channel_id=1, source_target_pairs={{0,15},{1,0},{2,1},{3,2},{4,3},{5,4},{6,5},{7,6},{8,7},{9,8},{10,9... | collective-permute-start | bytes 24584 | tf_op jit(solution)/shard_map/ppermute | solution.py:34
  43.9 1.6 collective-permute-done.4
  45.6 5.3 %collective-permute-start.7 = (bf16[32,128]{1,0:T(8,128)(2,1)S(1)}, bf16[32,128]{1,0:T(8,128)(2,1)S(1)}, u32[]{:S(2)}, u32[]{:S(2)}) collective-permute-start(bf16[32,128]{1,0:T(8,128)(2,1)S(1)} %collective-permute-done.5), channel_id=1, source_target_pairs={{0,15},{1,0},{2,1},{3,2},{4,3},{5,4},{6,5},{7,6},{8,7},{9,8},{10,9... | collective-permute-start | bytes 24584 | tf_op jit(solution)/shard_map/ppermute | solution.py:34
  50.9 1.6 collective-permute-done.6
  52.5 5.3 %collective-permute-start.9 = (bf16[32,128]{1,0:T(8,128)(2,1)S(1)}, bf16[32,128]{1,0:T(8,128)(2,1)S(1)}, u32[]{:S(2)}, u32[]{:S(2)}) collective-permute-start(bf16[32,128]{1,0:T(8,128)(2,1)S(1)} %collective-permute-done.7), channel_id=1, source_target_pairs={{0,15},{1,0},{2,1},{3,2},{4,3},{5,4},{6,5},{7,6},{8,7},{9,8},{10,9... | collective-permute-start | bytes 24584 | tf_op jit(solution)/shard_map/ppermute | solution.py:34
  57.9 1.6 collective-permute-done.8
  59.5 5.3 %collective-permute-start.11 = (bf16[32,128]{1,0:T(8,128)(2,1)S(1)}, bf16[32,128]{1,0:T(8,128)(2,1)S(1)}, u32[]{:S(2)}, u32[]{:S(2)}) collective-permute-start(bf16[32,128]{1,0:T(8,128)(2,1)S(1)} %collective-permute-done.9), channel_id=1, source_target_pairs={{0,15},{1,0},{2,1},{3,2},{4,3},{5,4},{6,5},{7,6},{8,7},{9,8},{10,9... | collective-permute-start | bytes 24584 | tf_op jit(solution)/shard_map/ppermute | solution.py:34
  64.9 1.6 collective-permute-done.10
  66.5 5.3 %collective-permute-start.13 = (bf16[32,128]{1,0:T(8,128)(2,1)S(1)}, bf16[32,128]{1,0:T(8,128)(2,1)S(1)}, u32[]{:S(2)}, u32[]{:S(2)}) collective-permute-start(bf16[32,128]{1,0:T(8,128)(2,1)S(1)} %collective-permute-done.11), channel_id=1, source_target_pairs={{0,15},{1,0},{2,1},{3,2},{4,3},{5,4},{6,5},{7,6},{8,7},{9,8},{10,9... | collective-permute-start | bytes 24584 | tf_op jit(solution)/shard_map/ppermute | solution.py:34
  71.8 1.6 collective-permute-done.12
  73.5 6.9 %collective-permute-done.14 = bf16[32,128]{1,0:T(8,128)(2,1)S(1)} collective-permute-done((bf16[32,128]{1,0:T(8,128)(2,1)S(1)}, bf16[32,128]{1,0:T(8,128)(2,1)S(1)}, u32[]{:S(2)}, u32[]{:S(2)}) %collective-permute-start.14) | collective-permute-done | bytes 8224 | tf_op jit(solution)/shard_map/ppermute | solution.py:29
  80.5 35.6 %while.13 = (s32[]{:T(128)}, f32[2048,128]{1,0:T(8,128)S(1)}, s32[]{:T(128)}, s32[5,3]{1,0:T(8,128)S(1)}, bf16[5,128,8192]{2,1,0:T(8,128)(2,1)}, /*index=5*/bf16...) while((s32[]{:T(128)}, f32[2048,128]{1,0:T(8,128)S(1)}, ...), condition=%wide.region_3.4_spmd, body=%wide.region_0.3_spmd.sunk | while | flops 270573568 | bytes 6799827 | solution.py:64
  81.2 6.3 %conditional.2 = (f32[2048,128]{1,0:T(8,128)S(1)}) conditional(s32[]{:T(128)} %convert_element_type.27, f32[2048,128]{1,0:T(8,128)S(1)} %get-tuple-element.150, (s32[]{:T(128)}, f32[2048,128]{1,0:T(8,128)S(1)}, s32[]{:T(128)}, bf16[5,128,8192]{2,1,0:T(8,128)(2,1)}, s32[1,3]{1,0:T(1,128)S(1)}, /*index=5*/bf16[2048,128]{1,0:T(8,128)(2,1)}, ...), branch_computations={%region_1.1_spmd, %region_2.2_spmd} | conditional | flops 270573568 | bytes 6799554 | solution.py:62
  82.5 0.8 dynamic-slice_convert_fusion
  84.6 2.3 %fusion.3 = f32[128,128]{1,0:T(8,128)S(1)} fusion(bf16[8192,128]{1,0:T(8,128)(2,1)S(1)} %bitcast.18, bf16[5,128,8192]{2,1,0:T(8,128)(2,1)} %get-tuple-element.54, s32[]{:T(128)S(6)} %select_n.90, f32[2048,128]{1,0:T(8,128)S(1)} %get-tuple-element.52, s32[]{:T(128)S(6)} %min.3), kind=kOutput, calls=%fused_computation.4 | convolution fusion | flops 268451840 | bytes 4325384 | tf_op jit(solution)/shard_map/while/body/cond/branch_1_fun/dot_general | solution.py:55
  88.2 6.3 %conditional.2 = (f32[2048,128]{1,0:T(8,128)S(1)}) conditional(s32[]{:T(128)} %convert_element_type.27, f32[2048,128]{1,0:T(8,128)S(1)} %get-tuple-element.150, (s32[]{:T(128)}, f32[2048,128]{1,0:T(8,128)S(1)}, s32[]{:T(128)}, bf16[5,128,8192]{2,1,0:T(8,128)(2,1)}, s32[1,3]{1,0:T(1,128)S(1)}, /*index=5*/bf16[2048,128]{1,0:T(8,128)(2,1)}, ...), branch_computations={%region_1.1_spmd, %region_2.2_spmd} | conditional | flops 270573568 | bytes 6799554 | solution.py:62
  89.5 0.8 dynamic-slice_convert_fusion
  91.6 2.3 %fusion.3 = f32[128,128]{1,0:T(8,128)S(1)} fusion(bf16[8192,128]{1,0:T(8,128)(2,1)S(1)} %bitcast.18, bf16[5,128,8192]{2,1,0:T(8,128)(2,1)} %get-tuple-element.54, s32[]{:T(128)S(6)} %select_n.90, f32[2048,128]{1,0:T(8,128)S(1)} %get-tuple-element.52, s32[]{:T(128)S(6)} %min.3), kind=kOutput, calls=%fused_computation.4 | convolution fusion | flops 268451840 | bytes 4325384 | tf_op jit(solution)/shard_map/while/body/cond/branch_1_fun/dot_general | solution.py:55
  95.2 6.3 %conditional.2 = (f32[2048,128]{1,0:T(8,128)S(1)}) conditional(s32[]{:T(128)} %convert_element_type.27, f32[2048,128]{1,0:T(8,128)S(1)} %get-tuple-element.150, (s32[]{:T(128)}, f32[2048,128]{1,0:T(8,128)S(1)}, s32[]{:T(128)}, bf16[5,128,8192]{2,1,0:T(8,128)(2,1)}, s32[1,3]{1,0:T(1,128)S(1)}, /*index=5*/bf16[2048,128]{1,0:T(8,128)(2,1)}, ...), branch_computations={%region_1.1_spmd, %region_2.2_spmd} | conditional | flops 270573568 | bytes 6799554 | solution.py:62
  96.5 0.8 dynamic-slice_convert_fusion
  98.6 2.3 %fusion.3 = f32[128,128]{1,0:T(8,128)S(1)} fusion(bf16[8192,128]{1,0:T(8,128)(2,1)S(1)} %bitcast.18, bf16[5,128,8192]{2,1,0:T(8,128)(2,1)} %get-tuple-element.54, s32[]{:T(128)S(6)} %select_n.90, f32[2048,128]{1,0:T(8,128)S(1)} %get-tuple-element.52, s32[]{:T(128)S(6)} %min.3), kind=kOutput, calls=%fused_computation.4 | convolution fusion | flops 268451840 | bytes 4325384 | tf_op jit(solution)/shard_map/while/body/cond/branch_1_fun/dot_general | solution.py:55
  102.2 6.3 %conditional.2 = (f32[2048,128]{1,0:T(8,128)S(1)}) conditional(s32[]{:T(128)} %convert_element_type.27, f32[2048,128]{1,0:T(8,128)S(1)} %get-tuple-element.150, (s32[]{:T(128)}, f32[2048,128]{1,0:T(8,128)S(1)}, s32[]{:T(128)}, bf16[5,128,8192]{2,1,0:T(8,128)(2,1)}, s32[1,3]{1,0:T(1,128)S(1)}, /*index=5*/bf16[2048,128]{1,0:T(8,128)(2,1)}, ...), branch_computations={%region_1.1_spmd, %region_2.2_spmd} | conditional | flops 270573568 | bytes 6799554 | solution.py:62
  105.6 2.3 %fusion.3 = f32[128,128]{1,0:T(8,128)S(1)} fusion(bf16[8192,128]{1,0:T(8,128)(2,1)S(1)} %bitcast.18, bf16[5,128,8192]{2,1,0:T(8,128)(2,1)} %get-tuple-element.54, s32[]{:T(128)S(6)} %select_n.90, f32[2048,128]{1,0:T(8,128)S(1)} %get-tuple-element.52, s32[]{:T(128)S(6)} %min.3), kind=kOutput, calls=%fused_computation.4 | convolution fusion | flops 268451840 | bytes 4325384 | tf_op jit(solution)/shard_map/while/body/cond/branch_1_fun/dot_general | solution.py:55
  109.2 6.3 %conditional.2 = (f32[2048,128]{1,0:T(8,128)S(1)}) conditional(s32[]{:T(128)} %convert_element_type.27, f32[2048,128]{1,0:T(8,128)S(1)} %get-tuple-element.150, (s32[]{:T(128)}, f32[2048,128]{1,0:T(8,128)S(1)}, s32[]{:T(128)}, bf16[5,128,8192]{2,1,0:T(8,128)(2,1)}, s32[1,3]{1,0:T(1,128)S(1)}, /*index=5*/bf16[2048,128]{1,0:T(8,128)(2,1)}, ...), branch_computations={%region_1.1_spmd, %region_2.2_spmd} | conditional | flops 270573568 | bytes 6799554 | solution.py:62
  112.6 2.3 %fusion.3 = f32[128,128]{1,0:T(8,128)S(1)} fusion(bf16[8192,128]{1,0:T(8,128)(2,1)S(1)} %bitcast.18, bf16[5,128,8192]{2,1,0:T(8,128)(2,1)} %get-tuple-element.54, s32[]{:T(128)S(6)} %select_n.90, f32[2048,128]{1,0:T(8,128)S(1)} %get-tuple-element.52, s32[]{:T(128)S(6)} %min.3), kind=kOutput, calls=%fused_computation.4 | convolution fusion | flops 268451840 | bytes 4325384 | tf_op jit(solution)/shard_map/while/body/cond/branch_1_fun/dot_general | solution.py:55
  116.2 1.0 copy-done
  117.2 75.7 %reduce-scatter.2.cloned.1.call-done = f32[128,128]{1,0:T(8,128)} async-done(((f32[2048,128]{1,0:T(8,128)}), f32[128,128]{1,0:T(8,128)}) %reduce-scatter.2.cloned.1.call-update) | async-done | bytes 65552 | tf_op jit(solution)/shard_map/reduce_scatter | solution.py:65
  (64 shorter events, 13.3 us)
Async XLA Ops:
  6.5 186.3 %reduce-scatter.2.cloned.1.call-start = ((), (), s32[]{:S(2)}) async-start(), calls=%async_computation.1 | async-start | bytes 1114112 | tf_op jit(solution)/shard_map/reduce_scatter | solution.py:65
  6.5 26.6 %collective-permute-start = (bf16[32,128]{1,0:T(8,128)(2,1)}, bf16[32,128]{1,0:T(8,128)(2,1)S(1)}, u32[]{:S(2)}, u32[]{:S(2)}) collective-permute-start(bf16[32,128]{1,0:T(8,128)(2,1)} %param.13), channel_id=1, source_target_pairs={{0,1},{1,2},{2,3},{3,4},{4,5},{5,6},{6,7},{7,8},{8,9},{9,10},{10,1... | collective-permute-start | bytes 24584 | tf_op jit(solution)/shard_map/ppermute | solution.py:29
  8.0 26.6 %collective-permute-start.1 = (bf16[32,128]{1,0:T(8,128)(2,1)}, bf16[32,128]{1,0:T(8,128)(2,1)S(1)}, u32[]{:S(2)}, u32[]{:S(2)}) collective-permute-start(bf16[32,128]{1,0:T(8,128)(2,1)} %param.13), channel_id=1, source_target_pairs={{0,15},{1,0},{2,1},{3,2},{4,3},{5,4},{6,5},{7,6},{8,7},{9,8},{10,9... | collective-permute-start | bytes 24584 | tf_op jit(solution)/shard_map/ppermute | solution.py:34
  33.1 5.5 %collective-permute-start.2 = (bf16[32,128]{1,0:T(8,128)(2,1)S(1)}, bf16[32,128]{1,0:T(8,128)(2,1)S(1)}, u32[]{:S(2)}, u32[]{:S(2)}) collective-permute-start(bf16[32,128]{1,0:T(8,128)(2,1)S(1)} %collective-permute-done), channel_id=1, source_target_pairs={{0,1},{1,2},{2,3},{3,4},{4,5},{5,6},{6,7},{7,8},{8,9},{9,10},{10,1... | collective-permute-start | bytes 24584 | tf_op jit(solution)/shard_map/ppermute | solution.py:29
  34.6 4.0 %collective-permute-start.3 = (bf16[32,128]{1,0:T(8,128)(2,1)S(1)}, bf16[32,128]{1,0:T(8,128)(2,1)S(1)}, u32[]{:S(2)}, u32[]{:S(2)}) collective-permute-start(bf16[32,128]{1,0:T(8,128)(2,1)S(1)} %collective-permute-done.1), channel_id=1, source_target_pairs={{0,15},{1,0},{2,1},{3,2},{4,3},{5,4},{6,5},{7,6},{8,7},{9,8},{10,9... | collective-permute-start | bytes 24584 | tf_op jit(solution)/shard_map/ppermute | solution.py:34
  38.6 7.0 %collective-permute-start.4 = (bf16[32,128]{1,0:T(8,128)(2,1)S(1)}, bf16[32,128]{1,0:T(8,128)(2,1)S(1)}, u32[]{:S(2)}, u32[]{:S(2)}) collective-permute-start(bf16[32,128]{1,0:T(8,128)(2,1)S(1)} %collective-permute-done.2), channel_id=1, source_target_pairs={{0,1},{1,2},{2,3},{3,4},{4,5},{5,6},{6,7},{7,8},{8,9},{9,10},{10,1... | collective-permute-start | bytes 24584 | tf_op jit(solution)/shard_map/ppermute | solution.py:29
  38.6 7.0 %collective-permute-start.5 = (bf16[32,128]{1,0:T(8,128)(2,1)S(1)}, bf16[32,128]{1,0:T(8,128)(2,1)S(1)}, u32[]{:S(2)}, u32[]{:S(2)}) collective-permute-start(bf16[32,128]{1,0:T(8,128)(2,1)S(1)} %collective-permute-done.3), channel_id=1, source_target_pairs={{0,15},{1,0},{2,1},{3,2},{4,3},{5,4},{6,5},{7,6},{8,7},{9,8},{10,9... | collective-permute-start | bytes 24584 | tf_op jit(solution)/shard_map/ppermute | solution.py:34
  45.6 7.0 %collective-permute-start.6 = (bf16[32,128]{1,0:T(8,128)(2,1)S(1)}, bf16[32,128]{1,0:T(8,128)(2,1)S(1)}, u32[]{:S(2)}, u32[]{:S(2)}) collective-permute-start(bf16[32,128]{1,0:T(8,128)(2,1)S(1)} %collective-permute-done.4), channel_id=1, source_target_pairs={{0,1},{1,2},{2,3},{3,4},{4,5},{5,6},{6,7},{7,8},{8,9},{9,10},{10,1... | collective-permute-start | bytes 24584 | tf_op jit(solution)/shard_map/ppermute | solution.py:29
  45.6 7.0 %collective-permute-start.7 = (bf16[32,128]{1,0:T(8,128)(2,1)S(1)}, bf16[32,128]{1,0:T(8,128)(2,1)S(1)}, u32[]{:S(2)}, u32[]{:S(2)}) collective-permute-start(bf16[32,128]{1,0:T(8,128)(2,1)S(1)} %collective-permute-done.5), channel_id=1, source_target_pairs={{0,15},{1,0},{2,1},{3,2},{4,3},{5,4},{6,5},{7,6},{8,7},{9,8},{10,9... | collective-permute-start | bytes 24584 | tf_op jit(solution)/shard_map/ppermute | solution.py:34
  52.5 7.0 %collective-permute-start.8 = (bf16[32,128]{1,0:T(8,128)(2,1)S(1)}, bf16[32,128]{1,0:T(8,128)(2,1)S(1)}, u32[]{:S(2)}, u32[]{:S(2)}) collective-permute-start(bf16[32,128]{1,0:T(8,128)(2,1)S(1)} %collective-permute-done.6), channel_id=1, source_target_pairs={{0,1},{1,2},{2,3},{3,4},{4,5},{5,6},{6,7},{7,8},{8,9},{9,10},{10,1... | collective-permute-start | bytes 24584 | tf_op jit(solution)/shard_map/ppermute | solution.py:29
  52.5 7.0 %collective-permute-start.9 = (bf16[32,128]{1,0:T(8,128)(2,1)S(1)}, bf16[32,128]{1,0:T(8,128)(2,1)S(1)}, u32[]{:S(2)}, u32[]{:S(2)}) collective-permute-start(bf16[32,128]{1,0:T(8,128)(2,1)S(1)} %collective-permute-done.7), channel_id=1, source_target_pairs={{0,15},{1,0},{2,1},{3,2},{4,3},{5,4},{6,5},{7,6},{8,7},{9,8},{10,9... | collective-permute-start | bytes 24584 | tf_op jit(solution)/shard_map/ppermute | solution.py:34
  59.5 7.0 %collective-permute-start.10 = (bf16[32,128]{1,0:T(8,128)(2,1)S(1)}, bf16[32,128]{1,0:T(8,128)(2,1)S(1)}, u32[]{:S(2)}, u32[]{:S(2)}) collective-permute-start(bf16[32,128]{1,0:T(8,128)(2,1)S(1)} %collective-permute-done.8), channel_id=1, source_target_pairs={{0,1},{1,2},{2,3},{3,4},{4,5},{5,6},{6,7},{7,8},{8,9},{9,10},{10,1... | collective-permute-start | bytes 24584 | tf_op jit(solution)/shard_map/ppermute | solution.py:29
  59.5 7.0 %collective-permute-start.11 = (bf16[32,128]{1,0:T(8,128)(2,1)S(1)}, bf16[32,128]{1,0:T(8,128)(2,1)S(1)}, u32[]{:S(2)}, u32[]{:S(2)}) collective-permute-start(bf16[32,128]{1,0:T(8,128)(2,1)S(1)} %collective-permute-done.9), channel_id=1, source_target_pairs={{0,15},{1,0},{2,1},{3,2},{4,3},{5,4},{6,5},{7,6},{8,7},{9,8},{10,9... | collective-permute-start | bytes 24584 | tf_op jit(solution)/shard_map/ppermute | solution.py:34
  66.5 7.0 %collective-permute-start.12 = (bf16[32,128]{1,0:T(8,128)(2,1)S(1)}, bf16[32,128]{1,0:T(8,128)(2,1)S(1)}, u32[]{:S(2)}, u32[]{:S(2)}) collective-permute-start(bf16[32,128]{1,0:T(8,128)(2,1)S(1)} %collective-permute-done.10), channel_id=1, source_target_pairs={{0,1},{1,2},{2,3},{3,4},{4,5},{5,6},{6,7},{7,8},{8,9},{9,10},{10,1... | collective-permute-start | bytes 24584 | tf_op jit(solution)/shard_map/ppermute | solution.py:29
  66.5 7.0 %collective-permute-start.13 = (bf16[32,128]{1,0:T(8,128)(2,1)S(1)}, bf16[32,128]{1,0:T(8,128)(2,1)S(1)}, u32[]{:S(2)}, u32[]{:S(2)}) collective-permute-start(bf16[32,128]{1,0:T(8,128)(2,1)S(1)} %collective-permute-done.11), channel_id=1, source_target_pairs={{0,15},{1,0},{2,1},{3,2},{4,3},{5,4},{6,5},{7,6},{8,7},{9,8},{10,9... | collective-permute-start | bytes 24584 | tf_op jit(solution)/shard_map/ppermute | solution.py:34
  73.4 7.0 %collective-permute-start.14 = (bf16[32,128]{1,0:T(8,128)(2,1)S(1)}, bf16[32,128]{1,0:T(8,128)(2,1)S(1)}, u32[]{:S(2)}, u32[]{:S(2)}) collective-permute-start(bf16[32,128]{1,0:T(8,128)(2,1)S(1)} %collective-permute-done.12), channel_id=1, source_target_pairs={{0,1},{1,2},{2,3},{3,4},{4,5},{5,6},{6,7},{7,8},{8,9},{9,10},{10,1... | collective-permute-start | bytes 24584 | tf_op jit(solution)/shard_map/ppermute | solution.py:29
  116.1 1.0 copy-start
Sparse Core Ops, SparseCore 0:
  117.3 75.5 reduce-scatter.1
